TPU v7x, 32 devices: a whole 2x2x4 slice. The times are simulated.
32 devices in a mesh: dom: 8 (over z, y), edge: 4 (over x, core).
Axes of the slice: x: 2, y: 2, z: 4, core: 2. Of those that a mesh axis runs over, the one named last changes fastest.
Arguments:
- fine_nodes: bfloat16 [65536, 128], P('dom'), may hold values from -6 to 6
- fine_edges: bfloat16 [131072, 128], P(('dom', 'edge')), may hold values from -6 to 6
- fine_senders: int32 [131072], P(('dom', 'edge')), may hold values from 0 to 8703, as said below
- fine_receivers: int32 [131072], P(('dom', 'edge')), may hold values from 0 to 8191
- fine_halo: int32 [8, 8, 64], P('dom'), may hold values from 0 to 8191
- coarse_edges: bfloat16 [32768, 128], P(('dom', 'edge')), may hold values from -6 to 6
- coarse_senders: int32 [32768], P(('dom', 'edge')), may hold values from 0 to 2303, as said below
- coarse_receivers: int32 [32768], P(('dom', 'edge')), may hold values from 0 to 2047
- coarse_halo: int32 [8, 8, 32], P('dom'), may hold values from 0 to 2047
- pool_send: int32 [8, 8, 1536], P('dom'), may hold values from 0 to 8191, as said below
- pool_dest: int32 [8, 8, 1536], P('dom'), may hold values from 0 to 2048, as said below
- unpool_slot: int32 [65536], P('dom'), may hold values from 0 to 12287, as said below
- edge_in_weight: bfloat16 [2, 384, 128], replicated, may hold values from -0.3125 to 0.3125
- edge_out_weight: bfloat16 [2, 128, 128], replicated, may hold values from -0.5 to 0.5
- node_in_weight: bfloat16 [2, 256, 128], replicated, may hold values from -0.375 to 0.375
- node_out_weight: bfloat16 [2, 128, 128], replicated, may hold values from -0.5 to 0.5
- edge_gain: float32 [2, 128], replicated, may hold values from 0.5 to 1.5
- node_gain: float32 [2, 128], replicated, may hold values from 0.5 to 1.5
Outputs:
- fine_out: bfloat16 [65536, 128], P('dom')
- coarse_out: bfloat16 [16384, 128], P('dom')
Inputs may be any that keep to these rules, and one draw needn't show every extreme that they name: `fine_senders`: an entry below 8192 is a row of the edge's own partition; an entry 8192 + d * 64 + s names slot s of fine_halo[d, p] for the edge's partition p. `coarse_senders`: an entry below 2048 is a row of the edge's own coarse partition; an entry 2048 + d * 32 + s names slot s of coarse_halo[d, p]. pool_send[d, p, s] is a row of partition d. For each pair (d, p) the slots that carry data come first and number at most 1536; in every draw some p receives 1536 from every d. Every row of partition d is carried exactly once over all p and s; empty slots hold 0. pool_dest[p, d, s] is 2048 exactly where slot s of pool_send[d, p] is empty, else a row of coarse partition p. `unpool_slot`: row r of partition d holds p * 1536 + s for the one carrying slot with pool_send[d, p, s] = r.
All inputs are finite; a program needn't handle non-finite values.
Results may differ from a plain program's by a relative error of at most 0.0068.
Values may be sent and summed in bfloat16 or wider, within the bound.
No kernel may reach another device: no remote copies, remote signals or barrier semaphores. Data moves between devices by JAX's collectives and lax.ppermute only.
A program may use at most 64 MiB of HBM per device.

v0:
```python
import jax
import jax.numpy as jnp
from jax import lax
from jax.sharding import PartitionSpec as P

COARSE = 2048


def layer_norm(values, gain):
    center = values - jnp.mean(values, axis=-1, keepdims=True)
    spread = jnp.mean(center * center, axis=-1, keepdims=True)
    return center * lax.rsqrt(spread + 1e-05) * gain


def node_update(rows, summed, w_first, w_second, gain):
    inputs = jnp.concatenate([rows, summed.astype(jnp.bfloat16)], axis=1)
    hidden = jax.nn.silu(jnp.dot(inputs, w_first, preferred_element_type=jnp.float32)).astype(
        jnp.bfloat16
    )
    result = layer_norm(jnp.dot(hidden, w_second, preferred_element_type=jnp.float32), gain)
    return (rows.astype(jnp.float32) + result).astype(jnp.bfloat16)


def graph_layer(nodes, edges, senders, receivers, border, level, weights):
    edge_in_weight, edge_out_weight, node_in_weight, node_out_weight, edge_gain, node_gain = weights
    width = nodes.shape[-1]
    outgoing = nodes[border[0]]
    ghosts = lax.all_to_all(outgoing, "dom", split_axis=0, concat_axis=0, tiled=True)
    table = jnp.concatenate([nodes, ghosts.reshape(-1, width)], axis=0)
    inputs = jnp.concatenate([table[senders], nodes[receivers], edges], axis=1)
    hidden = jax.nn.silu(
        jnp.dot(inputs, edge_in_weight[level], preferred_element_type=jnp.float32)
    ).astype(jnp.bfloat16)
    message = layer_norm(
        jnp.dot(hidden, edge_out_weight[level], preferred_element_type=jnp.float32),
        edge_gain[level],
    )
    partial_sum = jax.ops.segment_sum(message, receivers, num_segments=nodes.shape[0])
    summed = lax.psum(partial_sum, "edge")
    return node_update(
        nodes, summed, node_in_weight[level], node_out_weight[level], node_gain[level]
    )


def pooled_mean(arrived, places, width):
    sums = jax.ops.segment_sum(
        arrived.reshape(-1, width).astype(jnp.float32), places, num_segments=COARSE + 1
    )[:COARSE]
    counts = jax.ops.segment_sum(jnp.ones_like(places), places, num_segments=COARSE + 1)[:COARSE]
    return (sums / jnp.maximum(counts, 1).astype(jnp.float32)[:, None]).astype(jnp.bfloat16)


def shards(
    fine_nodes,
    fine_edges,
    fine_senders,
    fine_receivers,
    fine_halo,
    coarse_edges,
    coarse_senders,
    coarse_receivers,
    coarse_halo,
    pool_send,
    pool_dest,
    unpool_slot,
    edge_in_weight,
    edge_out_weight,
    node_in_weight,
    node_out_weight,
    edge_gain,
    node_gain,
):
    weights = (
        edge_in_weight,
        edge_out_weight,
        node_in_weight,
        node_out_weight,
        edge_gain,
        node_gain,
    )
    width = fine_nodes.shape[-1]
    fine_mid = graph_layer(
        fine_nodes, fine_edges, fine_senders, fine_receivers, fine_halo, 0, weights
    )
    places = pool_dest[0].reshape(-1)
    arrived = lax.all_to_all(fine_mid[pool_send[0]], "dom", split_axis=0, concat_axis=0, tiled=True)
    coarse_in = pooled_mean(arrived, places, width)
    coarse_out = graph_layer(
        coarse_in, coarse_edges, coarse_senders, coarse_receivers, coarse_halo, 1, weights
    )
    padded = jnp.concatenate([coarse_out, jnp.zeros((1, width), jnp.bfloat16)], axis=0)
    back = lax.all_to_all(padded[pool_dest[0]], "dom", split_axis=0, concat_axis=0, tiled=True)
    parents = back.reshape(-1, width)[unpool_slot]
    fine_out = (fine_mid.astype(jnp.float32) + parents.astype(jnp.float32)).astype(jnp.bfloat16)
    return (fine_out, coarse_out)


def solution(mesh):
    placed = (
        P("dom", None),
        P(("dom", "edge"), None),
        P(("dom", "edge")),
        P(("dom", "edge")),
        P("dom", None, None),
        P(("dom", "edge"), None),
        P(("dom", "edge")),
        P(("dom", "edge")),
        P("dom", None, None),
        P("dom", None, None),
        P("dom", None, None),
        P("dom"),
        P(),
        P(),
        P(),
        P(),
        P(),
        P(),
    )
    return jax.shard_map(
        shards,
        mesh=mesh,
        in_specs=placed,
        out_specs=(P("dom", None), P("dom", None)),
        check_vma=False,
    )
```

profile of v0, /device:TPU:0, one launch (start us, length us, event | category | flops | bytes accessed | tf_op | source)
XLA Modules:
  0.0 604.5 jit_solution(17450261135767377777)
XLA Ops:
  0.6 0.7 compare_select_fusion.8
  1.3 0.1 reshape.183
  1.4 3.5 gather_fusion
  4.9 7.3 %all-to-all-start = ((bf16[8,64,128]{2,1,0:T(8,128)(2,1)}), bf16[8,64,128]{2,1,0:T(8,128)(2,1)S(1)}, u32[]{:S(2)}, u32[]{:S(2)}) async-start(bf16[8,64,128]{2,1,0:T(8,128)(2,1)} %bitcast.1), calls=%async_computation | async-start | bytes 262144 | tf_op jit(solution)/shard_map/all_to_all | solution.py:28
  12.2 0.7 fusion.77
  13.0 0.8 slice_bitcast_fusion.1
  13.7 1.0 compare_select_fusion.1
  14.7 0.8 slice_bitcast_fusion
  15.5 4.1 copy.24
  19.5 12.1 %gather_fusion.2 = bf16[4096,128]{1,0:T(8,128)(2,1)S(1)} fusion(bf16[8192,128]{1,0:T(8,128)(2,1)S(1)} %copy-done, s32[4096]{0:T(1024)S(1)} %fusion.77), kind=kCustom, calls=%fused_computation.2 | custom fusion | bytes 2113536 | tf_op jit(solution)/shard_map/gather | solution.py:30
  31.7 0.0 copy-done.8
  31.7 0.0 all-to-all-done
  31.7 5.6 pad_maximum_fusion
  37.3 16.2 %gather_fusion.1 = bf16[4096,128]{1,0:T(8,128)(2,1)} fusion(bf16[8704,128]{1,0:T(8,128)(2,1)} %pad_maximum_fusion, s32[4096]{0:T(1024)S(1)} %fusion.76), kind=kCustom, calls=%fused_computation.1 | custom fusion | bytes 2113536 | tf_op jit(solution)/shard_map/gather | solution.py:30
  53.5 0.0 copy-done.15
  53.5 4.3 fusion.95
  57.8 2.0 multiply_reduce_fusion.1
  59.8 0.2 copy-done.4
  60.0 1.7 multiply_multiply_fusion
  61.7 2.9 copy.25
  64.6 24.8 %scatter_custom_fusion = f32[8192,128]{1,0:T(8,128)} fusion(s32[4096]{0:T(1024)} %param.21, f32[4096,128]{1,0:T(8,128)} %copy.25, f32[]{:T(128)} %constant.13.clone.1), kind=kCustom, calls=%fused_computation.33 | custom fusion | flops 524288 | bytes 4194816 | tf_op jit(solution)/shard_map/scatter-add | solution.py:38
  89.4 77.1 %all-reduce.3 = bf16[8192,128]{1,0:T(8,128)(2,1)} all-reduce(f32[8192,128]{1,0:T(8,128)} %scatter_custom_fusion), channel_id=1, replica_groups=mesh['dom'=8,'edge'=4] {'edge'}, use_global_device_ids=true, to_apply=%region_3.4 | all-reduce | flops 1048576 | bytes 6291456 | tf_op jit(solution)/shard_map/psum | solution.py:39
  166.5 0.0 copy-done.14
  166.5 5.8 fusion.100
  172.3 2.8 multiply_reduce_fusion
  175.1 0.6 copy-done.2
  175.7 3.8 add_convert_fusion.1
  179.5 3.2 copy.26
  182.7 43.3 %gather_fusion.3 = bf16[12288,128]{1,0:T(8,128)(2,1)} fusion(bf16[8192,128]{1,0:T(8,128)(2,1)S(1)} %copy.26, s32[12288]{0:T(1024)S(1)} %broadcast_clamp_fusion.1), kind=kCustom, calls=%fused_computation.3 | custom fusion | bytes 6340608 | tf_op jit(solution)/shard_map/gather | solution.py:86
  226.0 5.5 all-to-all-start.1
  231.6 0.0 copy-done.6
  231.6 0.1 reshape.215
  231.7 75.2 %scatter_custom_fusion.2 = s32[2049]{0:T(1024)S(1)} fusion(s32[12288]{0:T(1024)S(1)} %reshape.263, s32[12288]{0:T(1024)S(1)} %broadcast.163, s32[]{:T(128)} %constant.14.clone.1), kind=kCustom, calls=%fused_computation.101 | custom fusion | flops 12288 | bytes 8200 | tf_op jit(solution)/shard_map/scatter-add | solution.py:49
  307.0 0.0 all-to-all-done.1
  307.0 0.0 copy-start.11
  307.1 76.8 %scatter_custom_fusion.1 = f32[2049,128]{1,0:T(8,128)} fusion(s32[12288]{0:T(1024)S(1)} %reshape.263, bf16[12288,128]{1,0:T(8,128)(2,1)S(1)} %bitcast.78, f32[]{:T(128)} %constant.13.clone.1), kind=kCustom, calls=%fused_computation.13 | custom fusion | flops 3145728 | bytes 4194820 | tf_op jit(solution)/shard_map/scatter-add | solution.py:46
  383.8 1.6 fusion.24
  385.4 1.5 gather_fusion.4
  386.8 11.6 %all-to-all-start.2 = ((bf16[8,32,128]{2,1,0:T(8,128)(2,1)}), bf16[8,32,128]{2,1,0:T(8,128)(2,1)S(1)}, u32[]{:S(2)}, u32[]{:S(2)}) async-start(bf16[8,32,128]{2,1,0:T(8,128)(2,1)} %bitcast.13), calls=%async_computation.2 | async-start | bytes 131072 | tf_op jit(solution)/shard_map/all_to_all | solution.py:28
  398.5 3.2 gather_fusion.6
  401.7 0.0 copy-start.12
  401.7 0.0 copy-start.13
  401.7 0.0 copy-start.16
  401.8 3.6 all-to-all-done.2
  405.4 3.2 gather_fusion.5
  408.7 0.6 fusion.105
  409.3 0.1 multiply_reduce_fusion.3
  409.4 0.1 multiply_multiply_fusion.1
  409.5 0.0 copy-start.18
  409.5 0.2 copy.27
  409.7 6.3 %scatter_custom_fusion.3 = f32[2048,128]{1,0:T(8,128)S(1)} fusion(s32[1024]{0:T(1024)S(1)} %copy-done.11, f32[1024,128]{1,0:T(8,128)S(1)} %copy.27, f32[]{:T(128)} %constant.13.clone.1), kind=kCustom, calls=%fused_computation.61 | custom fusion | flops 131072 | bytes 1048580 | tf_op jit(solution)/shard_map/scatter-add | solution.py:38
  416.0 25.8 %all-reduce.4 = bf16[2048,128]{1,0:T(8,128)(2,1)S(1)} all-reduce(f32[2048,128]{1,0:T(8,128)S(1)} %scatter_custom_fusion.3), channel_id=1, replica_groups=mesh['dom'=8,'edge'=4] {'edge'}, use_global_device_ids=true, to_apply=%region_11.12 | all-reduce | flops 262144 | bytes 1572864 | tf_op jit(solution)/shard_map/psum | solution.py:39
  441.8 0.9 fusion.110
  442.7 0.6 multiply_reduce_fusion.2
  443.3 1.0 add_convert_fusion.2
  444.3 0.0 copy-start.5
  444.3 0.8 copy-done.5
  445.2 43.3 %gather_fusion.7 = bf16[12288,128]{1,0:T(8,128)(2,1)} fusion(bf16[2049,128]{1,0:T(8,128)(2,1)S(1)} %concatenate.27, s32[12288]{0:T(1024)S(1)} %broadcast_clamp_fusion), kind=kCustom, calls=%fused_computation.7 | custom fusion | bytes 6340608 | tf_op jit(solution)/shard_map/gather | solution.py:92
  488.5 3.8 all-to-all-start.3
  492.3 71.3 %all-to-all-done.3 = bf16[8,1536,128]{2,1,0:T(8,128)(2,1)S(1)} async-done(((bf16[8,1536,128]{2,1,0:T(8,128)(2,1)}), bf16[8,1536,128]{2,1,0:T(8,128)(2,1)S(1)}, u32[]{:S(2)}, u32[]{:S(2)}) %all-to-all-start.3) | async-done | bytes 3145760 | tf_op jit(solution)/shard_map/all_to_all | solution.py:92
  563.6 29.2 %gather_fusion.8 = bf16[8192,128]{1,0:T(8,128)(2,1)} fusion(bf16[12288,128]{1,0:T(8,128)(2,1)S(1)} %bitcast.77, s32[8192]{0:T(1024)S(1)} %fusion.67), kind=kCustom, calls=%fused_computation.8 | custom fusion | bytes 4227072 | tf_op jit(solution)/shard_map/gather | solution.py:93
  592.8 4.2 copy.28
  597.1 3.4 add_convert_fusion
  600.5 4.1 copy.29
  (50 shorter events, 0.3 us)
Async XLA Ops:
  4.9 26.8 %all-to-all-start = ((bf16[8,64,128]{2,1,0:T(8,128)(2,1)}), bf16[8,64,128]{2,1,0:T(8,128)(2,1)S(1)}, u32[]{:S(2)}, u32[]{:S(2)}) async-start(bf16[8,64,128]{2,1,0:T(8,128)(2,1)} %bitcast.1), calls=%async_computation | async-start | bytes 262144 | tf_op jit(solution)/shard_map/all_to_all | solution.py:28
  13.7 5.8 copy-start
  19.5 12.1 %copy-start.8 = (s32[4096]{0:T(1024)S(1)}, s32[4096]{0:T(1024)}, u32[]{:S(2)}) copy-start(s32[4096]{0:T(1024)} %param.20) | copy-start | bytes 49156
  37.3 16.2 %copy-start.15 = (bf16[2,128,128]{2,1,0:T(8,128)(2,1)S(1)}, bf16[2,128,128]{2,1,0:T(8,128)(2,1)}, u32[]{:S(2)}) copy-start(bf16[2,128,128]{2,1,0:T(8,128)(2,1)} %param.31) | copy-start | bytes 196612
  57.8 2.2 copy-start.4
  89.4 77.1 %copy-start.14 = (bf16[2,256,128]{2,1,0:T(8,128)(2,1)S(1)}, bf16[2,256,128]{2,1,0:T(8,128)(2,1)}, u32[]{:S(2)}) copy-start(bf16[2,256,128]{2,1,0:T(8,128)(2,1)} %param.32) | copy-start | bytes 393220
  89.4 77.1 %copy-start.17 = (bf16[2,128,128]{2,1,0:T(8,128)(2,1)S(1)}, bf16[2,128,128]{2,1,0:T(8,128)(2,1)}, u32[]{:S(2)}) copy-start(bf16[2,128,128]{2,1,0:T(8,128)(2,1)} %param.33) | copy-start | bytes 196612
  172.3 3.4 copy-start.2
  226.0 5.5 copy-start.6
  226.0 5.5 copy-start.9
  226.0 81.0 %copy-start.10 = (s32[1024]{0:T(1024)S(1)}, s32[1024]{0:T(1024)}, u32[]{:S(2)}) copy-start(s32[1024]{0:T(1024)} %param.24) | copy-start | bytes 12292
  226.0 81.0 %all-to-all-start.1 = ((bf16[8,1536,128]{2,1,0:T(8,128)(2,1)}), bf16[8,1536,128]{2,1,0:T(8,128)(2,1)S(1)}, u32[]{:S(2)}, u32[]{:S(2)}) async-start(bf16[8,1536,128]{2,1,0:T(8,128)(2,1)} %bitcast.79), calls=%async_computation.1 | async-start | bytes 6291456 | tf_op jit(solution)/shard_map/all_to_all | solution.py:86
  307.0 91.4 %copy-start.11 = (s32[1024]{0:T(1024)S(1)}, s32[1024]{0:T(1024)}, u32[]{:S(2)}) copy-start(s32[1024]{0:T(1024)} %param.25) | copy-start | bytes 12292
  386.8 18.5 %all-to-all-start.2 = ((bf16[8,32,128]{2,1,0:T(8,128)(2,1)}), bf16[8,32,128]{2,1,0:T(8,128)(2,1)S(1)}, u32[]{:S(2)}, u32[]{:S(2)}) async-start(bf16[8,32,128]{2,1,0:T(8,128)(2,1)} %bitcast.13), calls=%async_computation.2 | async-start | bytes 131072 | tf_op jit(solution)/shard_map/all_to_all | solution.py:28
  401.7 6.9 %copy-start.12 = (bf16[1024,128]{1,0:T(8,128)(2,1)S(1)}, bf16[1024,128]{1,0:T(8,128)(2,1)}, u32[]{:S(2)}) copy-start(bf16[1024,128]{1,0:T(8,128)(2,1)} %param.23) | copy-start | bytes 786436
  401.7 6.9 %copy-start.13 = (bf16[2,384,128]{2,1,0:T(8,128)(2,1)S(1)}, bf16[2,384,128]{2,1,0:T(8,128)(2,1)}, u32[]{:S(2)}) copy-start(bf16[2,384,128]{2,1,0:T(8,128)(2,1)} %param.30) | copy-start | bytes 589828
  401.7 6.9 %copy-start.16 = (bf16[2,128,128]{2,1,0:T(8,128)(2,1)S(1)}, bf16[2,128,128]{2,1,0:T(8,128)(2,1)}, u32[]{:S(2)}) copy-start(bf16[2,128,128]{2,1,0:T(8,128)(2,1)} %param.31) | copy-start | bytes 196612
  409.5 32.3 %copy-start.18 = (bf16[2,128,128]{2,1,0:T(8,128)(2,1)S(1)}, bf16[2,128,128]{2,1,0:T(8,128)(2,1)}, u32[]{:S(2)}) copy-start(bf16[2,128,128]{2,1,0:T(8,128)(2,1)} %param.33) | copy-start | bytes 196612
  441.8 1.5 copy-start.3
  444.3 0.8 copy-start.5
  488.5 3.8 copy-start.7
  488.5 75.1 %all-to-all-start.3 = ((bf16[8,1536,128]{2,1,0:T(8,128)(2,1)}), bf16[8,1536,128]{2,1,0:T(8,128)(2,1)S(1)}, u32[]{:S(2)}, u32[]{:S(2)}) async-start(bf16[8,1536,128]{2,1,0:T(8,128)(2,1)} %bitcast.80), calls=%async_computation.3 | async-start | bytes 6291456 | tf_op jit(solution)/shard_map/all_to_all | solution.py:92
  592.8 4.2 copy-start.1
where the time goes:
time: 606 us; the launch traced here: 605 us
  other arithmetic  208 us (34%)
  local copies, waits for them, and re-layouts  178 us (29%)
  blocking collectives  103 us (17%)
  waiting for transfers between devices  74.9 us (12%)
  starting transfers between devices  28.2 us (5%)
  matrix products  11.6 us (2%)
    psum x2, blocking collectives, graph_layer(): summed = lax.psum(partial_sum, 'edge')  103 us
    scatter-add x1, other arithmetic, pooled_mean(): jax.ops.segment_sum(arrived.reshape(-1, width).astype(jnp.float32), place...  76.8 us
    scatter-add x1, other arithmetic, pooled_mean(): jax.ops.segment_sum(jnp.ones_like(places), places, num_segments=COARSE + 1)  75.2 us
    all_to_all x1, waiting for transfers between devices, shards(): lax.all_to_all(padded[pool_dest[0]], 'dom', split_axis=0, concat_axis=0,...  71.3 us
    gather x1, local copies, waits for them, and re-layouts, shards(): padded[pool_dest[0]]  43.3 us
    gather x1, local copies, waits for them, and re-layouts, shards(): fine_mid[pool_send[0]]  43.3 us
    gather x4, local copies, waits for them, and re-layouts, graph_layer(): inputs = jnp.concatenate([table[senders], nodes[receivers], edges], axis=1)  34.7 us
    gather x2, local copies, waits for them, and re-layouts, shards(): parents = back.reshape(-1, width)[unpool_slot]  33.5 us
  transfers between devices with their start and end apart: 4, of which 2 were waited for; matrix products, arithmetic and copies ran while one was open for 16% of the time, Pallas kernels for 0%

commit v1 on v0

--- a/solution.py
+++ b/solution.py
@@ -36,7 +36,8 @@
         edge_gain[level],
     )
     partial_sum = jax.ops.segment_sum(message, receivers, num_segments=nodes.shape[0])
-    summed = lax.psum(partial_sum, "edge")
+    pieces = lax.all_gather(partial_sum, "edge")
+    summed = jnp.sum(pieces, axis=0)
     return node_update(
         nodes, summed, node_in_weight[level], node_out_weight[level], node_gain[level]
     )

time: 606 us -> 665 us (1.097)
  waiting for transfers between devices: 74.9 us -> 210 us
  blocking collectives: 103 us -> 0 us
  between operations: 1.07 us -> 14.5 us
  other arithmetic: 208 us -> 219 us
    all_gather x0 -> x2, waiting for transfers between devices: none -> 136 us  [graph_layer(): pieces = lax.all_gather(partial_sum, 'edge')]
    psum x2 -> x0, blocking collectives: 103 us -> none  [graph_layer(): summed = lax.psum(partial_sum, 'edge')]
    reduce_sum x0 -> x2, other arithmetic: none -> 11.2 us  [graph_layer(): summed = jnp.sum(pieces, axis=0)]
  transfers between devices with their start and end apart: 4 -> 6, of which waited for: 2 -> 4; matrix products, arithmetic and copies ran while one was open for 16% -> 14% of each run, Pallas kernels for 0% -> 0%
where the time goes in v1:
time: 665 us; the launch traced here: 664 us
  other arithmetic  219 us (33%)
  waiting for transfers between devices  210 us (32%)
  local copies, waits for them, and re-layouts  178 us (27%)
  starting transfers between devices  30.5 us (5%)
  between operations  14.5 us (2%)
  matrix products  11.5 us (2%)
    all_gather x2, waiting for transfers between devices, graph_layer(): pieces = lax.all_gather(partial_sum, 'edge')  136 us
    scatter-add x1, other arithmetic, pooled_mean(): jax.ops.segment_sum(arrived.reshape(-1, width).astype(jnp.float32), place...  76.7 us
    scatter-add x1, other arithmetic, pooled_mean(): jax.ops.segment_sum(jnp.ones_like(places), places, num_segments=COARSE + 1)  75.2 us
    all_to_all x1, waiting for transfers between devices, shards(): lax.all_to_all(padded[pool_dest[0]], 'dom', split_axis=0, concat_axis=0,...  71.1 us
    gather x1, local copies, waits for them, and re-layouts, shards(): padded[pool_dest[0]]  43.6 us
    gather x1, local copies, waits for them, and re-layouts, shards(): fine_mid[pool_send[0]]  43.6 us
    gather x4, local copies, waits for them, and re-layouts, graph_layer(): inputs = jnp.concatenate([table[senders], nodes[receivers], edges], axis=1)  35.7 us
    gather x2, local copies, waits for them, and re-layouts, shards(): parents = back.reshape(-1, width)[unpool_slot]  33.7 us
  transfers between devices with their start and end apart: 6, of which 4 were waited for; matrix products, arithmetic and copies ran while one was open for 14% of the time, Pallas kernels for 0%

profile of v1, /device:TPU:0, one launch (start us, length us, event | category | flops | bytes accessed | tf_op | source)
XLA Modules:
  0.0 663.7 jit_solution(4371880036239416877)
XLA Ops:
  7.2 0.7 compare_select_fusion.8
  7.9 0.1 reshape.183
  7.9 3.5 gather_fusion
  11.5 7.3 %all-to-all-start = ((bf16[8,64,128]{2,1,0:T(8,128)(2,1)}), bf16[8,64,128]{2,1,0:T(8,128)(2,1)S(1)}, u32[]{:S(2)}, u32[]{:S(2)}) async-start(bf16[8,64,128]{2,1,0:T(8,128)(2,1)} %bitcast.1), calls=%async_computation | async-start | bytes 262144 | tf_op jit(solution)/shard_map/all_to_all | solution.py:28
  18.8 0.0 all-gather.5.cloned.1.call-start
  18.8 0.7 fusion.77
  19.5 0.8 slice_bitcast_fusion.1
  20.3 13.0 %gather_fusion.2 = bf16[4096,128]{1,0:T(8,128)(2,1)S(1)} fusion(bf16[8192,128]{1,0:T(8,128)(2,1)} %param.18, s32[4096]{0:T(1024)S(1)} %fusion.77), kind=kCustom, calls=%fused_computation.2 | custom fusion | bytes 2113536 | tf_op jit(solution)/shard_map/gather | solution.py:30
  33.4 0.0 all-to-all-done
  33.4 5.6 pad_maximum_fusion
  39.0 16.3 %gather_fusion.1 = bf16[4096,128]{1,0:T(8,128)(2,1)} fusion(bf16[8704,128]{1,0:T(8,128)(2,1)} %pad_maximum_fusion, s32[4096]{0:T(1024)S(1)} %fusion.76), kind=kCustom, calls=%fused_computation.1 | custom fusion | bytes 2113536 | tf_op jit(solution)/shard_map/gather | solution.py:30
  55.2 4.3 fusion.95
  59.5 2.0 multiply_reduce_fusion.1
  61.5 0.2 copy-done.4
  61.7 1.6 multiply_multiply_fusion
  63.4 2.9 copy.25
  66.3 24.8 %scatter_custom_fusion = f32[8192,128]{1,0:T(8,128)} fusion(s32[4096]{0:T(1024)} %param.21, f32[4096,128]{1,0:T(8,128)} %copy.25, f32[]{:T(128)} %constant.13.clone.1), kind=kCustom, calls=%fused_computation.33 | custom fusion | flops 524288 | bytes 4194816 | tf_op jit(solution)/shard_map/scatter-add | solution.py:38
  91.1 0.0 all-gather.5.cloned.1.call-update
  91.1 0.0 copy-start.7
  91.1 0.0 copy-start.13
  91.2 2.9 copy.24
  94.1 104.4 %all-gather.5.cloned.1.call-done = f32[32768,128]{1,0:T(8,128)} async-done(((f32[8192,128]{1,0:T(8,128)}), f32[32768,128]{1,0:T(8,128)}) %all-gather.5.cloned.1.call-update) | async-done | bytes 16777232 | tf_op jit(solution)/shard_map/all_gather | solution.py:39
  198.6 8.7 %reduce_sum.92 = bf16[8192,128]{1,0:T(8,128)(2,1)} reduce(f32[4,8192,128]{2,1,0:T(8,128)} %bitcast.80, f32[]{:T(128)} %constant.13.clone.1), dimensions={0}, to_apply=%region_3.4 | reduce | flops 3145728 | bytes 18874372 | tf_op jit(solution)/shard_map/reduce_sum | solution.py:40
  207.3 5.8 fusion.100
  213.1 2.8 multiply_reduce_fusion
  215.9 0.6 copy-done.2
  216.5 3.8 add_convert_fusion.1
  220.3 3.2 copy.26
  223.5 43.6 %gather_fusion.3 = bf16[12288,128]{1,0:T(8,128)(2,1)} fusion(bf16[8192,128]{1,0:T(8,128)(2,1)S(1)} %copy.26, s32[12288]{0:T(1024)S(1)} %broadcast_clamp_fusion.1), kind=kCustom, calls=%fused_computation.3 | custom fusion | bytes 6340608 | tf_op jit(solution)/shard_map/gather | solution.py:87
  267.2 5.7 all-to-all-start.1
  272.9 0.1 reshape.215
  272.9 75.2 %scatter_custom_fusion.2 = s32[2049]{0:T(1024)S(1)} fusion(s32[12288]{0:T(1024)S(1)} %reshape.263, s32[12288]{0:T(1024)S(1)} %broadcast.163, s32[]{:T(128)} %constant.14.clone.1), kind=kCustom, calls=%fused_computation.101 | custom fusion | flops 12288 | bytes 8200 | tf_op jit(solution)/shard_map/scatter-add | solution.py:50
  348.2 0.0 all-to-all-done.1
  348.2 0.0 copy-start.12
  348.3 76.7 %scatter_custom_fusion.1 = f32[2049,128]{1,0:T(8,128)} fusion(s32[12288]{0:T(1024)S(1)} %reshape.263, bf16[12288,128]{1,0:T(8,128)(2,1)S(1)} %bitcast.81, f32[]{:T(128)} %constant.13.clone.1), kind=kCustom, calls=%fused_computation.13 | custom fusion | flops 3145728 | bytes 4194820 | tf_op jit(solution)/shard_map/scatter-add | solution.py:47
  425.0 1.6 fusion.24
  426.6 1.5 gather_fusion.4
  428.0 11.6 %all-to-all-start.2 = ((bf16[8,32,128]{2,1,0:T(8,128)(2,1)}), bf16[8,32,128]{2,1,0:T(8,128)(2,1)S(1)}, u32[]{:S(2)}, u32[]{:S(2)}) async-start(bf16[8,32,128]{2,1,0:T(8,128)(2,1)} %bitcast.14), calls=%async_computation.2 | async-start | bytes 131072 | tf_op jit(solution)/shard_map/all_to_all | solution.py:28
  439.7 0.3 all-gather.7.cloned.1.call-start
  440.0 3.2 gather_fusion.6
  443.2 0.0 copy-start.14
  443.2 0.0 copy-start.19
  443.2 3.4 all-to-all-done.2
  446.6 3.2 gather_fusion.5
  449.9 0.6 fusion.105
  450.5 0.1 multiply_reduce_fusion.3
  450.6 0.1 multiply_multiply_fusion.1
  450.7 0.2 copy.27
  450.9 7.0 %scatter_custom_fusion.3 = f32[2048,128]{1,0:T(8,128)} fusion(s32[1024]{0:T(1024)S(1)} %copy-done.12, f32[1024,128]{1,0:T(8,128)S(1)} %copy.27, f32[]{:T(128)} %constant.13.clone.1), kind=kCustom, calls=%fused_computation.61 | custom fusion | flops 131072 | bytes 1048580 | tf_op jit(solution)/shard_map/scatter-add | solution.py:38
  457.9 0.0 all-gather.7.cloned.1.call-update
  458.0 31.4 %all-gather.7.cloned.1.call-done = f32[8192,128]{1,0:T(8,128)} async-done(((f32[2048,128]{1,0:T(8,128)}), f32[8192,128]{1,0:T(8,128)}) %all-gather.7.cloned.1.call-update) | async-done | bytes 4194320 | tf_op jit(solution)/shard_map/all_gather | solution.py:39
  489.4 2.5 reduce_sum.97
  491.9 0.9 fusion.110
  492.8 0.6 multiply_reduce_fusion.2
  493.5 1.0 add_convert_fusion.2
  494.5 0.0 copy-start.5
  494.5 0.8 copy-done.5
  495.3 43.6 %gather_fusion.7 = bf16[12288,128]{1,0:T(8,128)(2,1)} fusion(bf16[2049,128]{1,0:T(8,128)(2,1)S(1)} %concatenate.27, s32[12288]{0:T(1024)S(1)} %broadcast_clamp_fusion), kind=kCustom, calls=%fused_computation.7 | custom fusion | bytes 6340608 | tf_op jit(solution)/shard_map/gather | solution.py:93
  539.0 5.6 all-to-all-start.3
  544.6 71.1 %all-to-all-done.3 = bf16[8,1536,128]{2,1,0:T(8,128)(2,1)S(1)} async-done(((bf16[8,1536,128]{2,1,0:T(8,128)(2,1)}), bf16[8,1536,128]{2,1,0:T(8,128)(2,1)S(1)}, u32[]{:S(2)}, u32[]{:S(2)}) %all-to-all-start.3) | async-done | bytes 3145760 | tf_op jit(solution)/shard_map/all_to_all | solution.py:93
  615.7 29.4 %gather_fusion.8 = bf16[8192,128]{1,0:T(8,128)(2,1)} fusion(bf16[12288,128]{1,0:T(8,128)(2,1)S(1)} %bitcast.79, s32[8192]{0:T(1024)S(1)} %fusion.67), kind=kCustom, calls=%fused_computation.8 | custom fusion | bytes 4227072 | tf_op jit(solution)/shard_map/gather | solution.py:94
  645.1 4.2 copy.28
  649.4 3.4 add_convert_fusion
  652.8 4.1 copy.29
  (62 shorter events, 0.3 us)
Async XLA Ops:
  11.5 21.9 %all-to-all-start = ((bf16[8,64,128]{2,1,0:T(8,128)(2,1)}), bf16[8,64,128]{2,1,0:T(8,128)(2,1)S(1)}, u32[]{:S(2)}, u32[]{:S(2)}) async-start(bf16[8,64,128]{2,1,0:T(8,128)(2,1)} %bitcast.1), calls=%async_computation | async-start | bytes 262144 | tf_op jit(solution)/shard_map/all_to_all | solution.py:28
  18.8 179.8 %all-gather.5.cloned.1.call-start = ((), (), s32[]{:S(2)}) async-start(), calls=%async_computation.4 | async-start | bytes 20971520 | tf_op jit(solution)/shard_map/all_gather | solution.py:39
  20.3 13.0 %copy-start.9 = (s32[4096]{0:T(1024)S(1)}, s32[4096]{0:T(1024)}, u32[]{:S(2)}) copy-start(s32[4096]{0:T(1024)} %param.20) | copy-start | bytes 49156
  20.3 13.1 %copy-start = (bf16[8192,128]{1,0:T(8,128)(2,1)S(1)}, bf16[8192,128]{1,0:T(8,128)(2,1)}, u32[]{:S(2)}) copy-start(bf16[8192,128]{1,0:T(8,128)(2,1)} %param.18) | copy-start | bytes 6291460
  39.0 16.3 %copy-start.15 = (bf16[2,384,128]{2,1,0:T(8,128)(2,1)S(1)}, bf16[2,384,128]{2,1,0:T(8,128)(2,1)}, u32[]{:S(2)}) copy-start(bf16[2,384,128]{2,1,0:T(8,128)(2,1)} %param.30) | copy-start | bytes 589828
  39.0 16.3 %copy-start.18 = (bf16[2,128,128]{2,1,0:T(8,128)(2,1)S(1)}, bf16[2,128,128]{2,1,0:T(8,128)(2,1)}, u32[]{:S(2)}) copy-start(bf16[2,128,128]{2,1,0:T(8,128)(2,1)} %param.31) | copy-start | bytes 196612
  59.5 2.2 copy-start.4
  91.1 2.9 copy-start.7
  91.1 2.9 copy-start.13
  198.6 8.7 %copy-start.16 = (bf16[2,256,128]{2,1,0:T(8,128)(2,1)S(1)}, bf16[2,256,128]{2,1,0:T(8,128)(2,1)}, u32[]{:S(2)}) copy-start(bf16[2,256,128]{2,1,0:T(8,128)(2,1)} %param.32) | copy-start | bytes 393220
  198.6 8.7 %copy-start.20 = (bf16[2,128,128]{2,1,0:T(8,128)(2,1)S(1)}, bf16[2,128,128]{2,1,0:T(8,128)(2,1)}, u32[]{:S(2)}) copy-start(bf16[2,128,128]{2,1,0:T(8,128)(2,1)} %param.33) | copy-start | bytes 196612
  213.1 3.4 copy-start.2
  267.1 5.7 copy-start.6
  267.2 5.7 copy-start.10
  267.2 81.1 %copy-start.11 = (s32[1024]{0:T(1024)S(1)}, s32[1024]{0:T(1024)}, u32[]{:S(2)}) copy-start(s32[1024]{0:T(1024)} %param.24) | copy-start | bytes 12292
  267.2 81.1 %all-to-all-start.1 = ((bf16[8,1536,128]{2,1,0:T(8,128)(2,1)}), bf16[8,1536,128]{2,1,0:T(8,128)(2,1)S(1)}, u32[]{:S(2)}, u32[]{:S(2)}) async-start(bf16[8,1536,128]{2,1,0:T(8,128)(2,1)} %bitcast.82), calls=%async_computation.1 | async-start | bytes 6291456 | tf_op jit(solution)/shard_map/all_to_all | solution.py:87
  348.2 91.7 %copy-start.12 = (s32[1024]{0:T(1024)S(1)}, s32[1024]{0:T(1024)}, u32[]{:S(2)}) copy-start(s32[1024]{0:T(1024)} %param.25) | copy-start | bytes 12292
  428.0 18.5 %all-to-all-start.2 = ((bf16[8,32,128]{2,1,0:T(8,128)(2,1)}), bf16[8,32,128]{2,1,0:T(8,128)(2,1)S(1)}, u32[]{:S(2)}, u32[]{:S(2)}) async-start(bf16[8,32,128]{2,1,0:T(8,128)(2,1)} %bitcast.14), calls=%async_computation.2 | async-start | bytes 131072 | tf_op jit(solution)/shard_map/all_to_all | solution.py:28
  439.7 49.7 %all-gather.7.cloned.1.call-start = ((), (), s32[]{:S(2)}) async-start(), calls=%async_computation.5 | async-start | bytes 5242880 | tf_op jit(solution)/shard_map/all_gather | solution.py:39
  443.2 6.7 %copy-start.14 = (bf16[1024,128]{1,0:T(8,128)(2,1)S(1)}, bf16[1024,128]{1,0:T(8,128)(2,1)}, u32[]{:S(2)}) copy-start(bf16[1024,128]{1,0:T(8,128)(2,1)} %param.23) | copy-start | bytes 786436
  443.2 6.7 %copy-start.19 = (bf16[2,128,128]{2,1,0:T(8,128)(2,1)S(1)}, bf16[2,128,128]{2,1,0:T(8,128)(2,1)}, u32[]{:S(2)}) copy-start(bf16[2,128,128]{2,1,0:T(8,128)(2,1)} %param.31) | copy-start | bytes 196612
  489.4 2.5 copy-start.17
  489.4 2.5 copy-start.21
  491.9 1.5 copy-start.3
  494.5 0.8 copy-start.5
  539.0 5.7 copy-start.8
  539.0 76.8 %all-to-all-start.3 = ((bf16[8,1536,128]{2,1,0:T(8,128)(2,1)}), bf16[8,1536,128]{2,1,0:T(8,128)(2,1)S(1)}, u32[]{:S(2)}, u32[]{:S(2)}) async-start(bf16[8,1536,128]{2,1,0:T(8,128)(2,1)} %bitcast.83), calls=%async_computation.3 | async-start | bytes 6291456 | tf_op jit(solution)/shard_map/all_to_all | solution.py:93
  645.1 4.3 copy-start.1
Sparse Core Ops, SparseCore 0:
  91.3 107.2 all-gather.4
  458.1 31.3 all-gather.6
